TPU v7x, 32 devices: a whole 2x2x4 slice. The times are simulated.
32 devices in a mesh: head: 2 (over y), seq: 16 (over z, x, core).
Axes of the slice: x: 2, y: 2, z: 4, core: 2. Of those that a mesh axis runs over, the one named last changes fastest.
Arguments:
- queries: bfloat16 [2048, 4096], P(('seq', 'head')), may hold values from -20 to 20
- keys: bfloat16 [2048, 1024], P(('seq', 'head')), may hold values from -5 to 5
- values: bfloat16 [2048, 1024], P(('seq', 'head')), may hold values from -6 to 6
Outputs:
- attended: bfloat16 [2048, 4096], P(('seq', 'head'))
All inputs are finite; a program needn't handle non-finite values.
Results may differ from a plain program's by a relative error of at most 0.0041.
Values may be sent and summed in bfloat16 or wider, within the bound.
No kernel may reach another device: no remote copies, remote signals or barrier semaphores. Data moves between devices by JAX's collectives and lax.ppermute only.
A program may use at most 64 MiB of HBM per device.

v0:
```python
import math
import jax
import jax.numpy as jnp
from jax import lax
from jax.sharding import PartitionSpec as P

HEAD_DIM = 128


def update_state(state, query_half, query_pos, key_piece, value_piece, key_pos):
    largest, total, summed = state
    score = jnp.einsum("tkgd,pkd->tkgp", query_half, key_piece, preferred_element_type=jnp.float32)
    score = score / math.sqrt(query_half.shape[-1])
    allowed = (key_pos[None, :] <= query_pos[:, None])[:, None, None, :]
    score = jnp.where(allowed, score, jnp.float32(-1e30))
    new_largest = jnp.maximum(largest, jnp.max(score, axis=-1))
    weight = jnp.where(allowed, jnp.exp(score - new_largest[..., None]), jnp.float32(0.0))
    total = jnp.sum(weight, axis=-1)
    product = jnp.einsum(
        "tkgp,pkd->tkgd",
        weight.astype(jnp.bfloat16),
        value_piece,
        preferred_element_type=jnp.float32,
    )
    summed = product
    return (new_largest, total, summed)


def on_device(queries, keys, values):
    q_local, k_local, v_local = (
        lax.all_to_all(queries, "head", split_axis=1, concat_axis=0, tiled=True),
        lax.all_to_all(keys, "head", split_axis=1, concat_axis=0, tiled=True),
        lax.all_to_all(values, "head", split_axis=1, concat_axis=0, tiled=True),
    )
    tokens = q_local.shape[0]
    half = tokens // 2
    kv_local = k_local.shape[1] // HEAD_DIM
    group = q_local.shape[1] // k_local.shape[1]
    index = lax.axis_index("seq")
    offsets = jnp.arange(half, dtype=jnp.int32)
    later = q_local[half:]
    early_pos = index * tokens + offsets
    later_pos = index * tokens + half + offsets
    query_pos = jnp.stack([early_pos, later_pos])
    halves = jnp.stack([q_local[:half], later]).reshape(2, half, kv_local, group, HEAD_DIM)
    start_state = (
        jnp.full((2, half, kv_local, group), -1e30, jnp.float32),
        jnp.zeros((2, half, kv_local, group), jnp.float32),
        jnp.zeros((2, half, kv_local, group, HEAD_DIM), jnp.float32),
    )
    start = jnp.int32(0)
    key_piece = lax.all_gather(k_local, "seq", axis=0, tiled=True)
    value_piece = lax.all_gather(v_local, "seq", axis=0, tiled=True)
    rows = key_piece.shape[0]
    key_piece = key_piece.reshape(rows, kv_local, HEAD_DIM)
    value_piece = value_piece.reshape(rows, kv_local, HEAD_DIM)
    key_pos = jnp.arange(rows, dtype=jnp.int32)
    results = []
    for which in range(2):
        state = (start_state[0][which], start_state[1][which], start_state[2][which])
        needed = start <= query_pos[which, half - 1]

        def run(current, which=which):
            return update_state(
                current, halves[which], query_pos[which], key_piece, value_piece, key_pos
            )

        def keep(current):
            return current

        results.append(lax.cond(needed, run, keep, state))
    total = jnp.stack([results[0][1], results[1][1]])
    summed = jnp.stack([results[0][2], results[1][2]])
    result = (summed / total[..., None]).reshape(2, half, q_local.shape[1]).astype(jnp.bfloat16)
    later_out = result[1]
    combined = jnp.concatenate([result[0], later_out], axis=0)
    return lax.all_to_all(combined, "head", split_axis=0, concat_axis=1, tiled=True)


def solution(mesh):
    return jax.shard_map(
        on_device,
        mesh=mesh,
        in_specs=(P(("seq", "head"), None), P(("seq", "head"), None), P(("seq", "head"), None)),
        out_specs=P(("seq", "head"), None),
        check_vma=False,
    )
```

profile of v0, /device:TPU:0, one launch (start us, length us, event | category | flops | bytes accessed | tf_op | source)
XLA Modules:
  0.0 142.9 jit_solution(106555980706747682)
XLA Ops:
  6.5 0.9 copy.81
  7.5 8.6 %all_to_all.73 = bf16[64,2,512]{2,0,1:T(8,128)(2,1)} all-to-all(bf16[64,2,512]{2,0,1:T(8,128)(2,1)S(1)} %bitcast.111), channel_id=1, replica_groups=mesh['head'=2,'seq'=16] {'head'}, dimensions={1} | all-to-all | bytes 262144 | tf_op jit(solution)/shard_map/all_to_all | solution.py:32
  16.2 0.9 copy.80
  17.1 7.5 %all_to_all.74 = bf16[64,2,512]{2,0,1:T(8,128)(2,1)} all-to-all(bf16[64,2,512]{2,0,1:T(8,128)(2,1)S(1)} %bitcast.112), channel_id=1, replica_groups=mesh['head'=2,'seq'=16] {'head'}, dimensions={1} | all-to-all | bytes 262144 | tf_op jit(solution)/shard_map/all_to_all | solution.py:33
  24.6 1.9 %copy.79 = bf16[8,2,8,2048]{3,2,0,1:T(8,128)(2,1)} copy(bf16[8,2,8,2048]{3,2,1,0:T(8,128)(2,1)} %bitcast.108) | data formatting | bytes 1048576 | tf_op jit(solution)/shard_map/all_to_all | solution.py:31
  26.5 3.5 %all-to-all-start = ((bf16[64,2,2048]{2,0,1:T(8,128)(2,1)}), bf16[64,2,2048]{2,0,1:T(8,128)(2,1)S(1)}, u32[]{:S(2)}, u32[]{:S(2)}) async-start(bf16[64,2,2048]{2,0,1:T(8,128)(2,1)} %bitcast.98), calls=%async_computation | async-start | bytes 1048576 | tf_op jit(solution)/shard_map/all_to_all | solution.py:31
  32.6 4.0 %all-to-all-done = bf16[64,2,2048]{2,0,1:T(8,128)(2,1)S(1)} async-done(((bf16[64,2,2048]{2,0,1:T(8,128)(2,1)}), bf16[64,2,2048]{2,0,1:T(8,128)(2,1)S(1)}, u32[]{:S(2)}, u32[]{:S(2)}) %all-to-all-start) | async-done | bytes 524320 | tf_op jit(solution)/shard_map/all_to_all | solution.py:31
  37.2 21.2 %all-gather.3.cloned.1.call-done = bf16[2048,512]{1,0:T(8,128)(2,1)} async-done(((bf16[128,512]{1,0:T(8,128)(2,1)}), bf16[2048,512]{1,0:T(8,128)(2,1)}) %all-gather.3.cloned.1.call-update) | async-done | bytes 2097168 | tf_op jit(solution)/shard_map/all_gather | solution.py:52
  58.4 2.9 %copy.49 = bf16[2048,512]{0,1:T(8,128)(2,1)S(1)} copy(bf16[2048,512]{1,0:T(8,128)(2,1)} %all-gather.3.cloned.1.call-done) | data formatting | bytes 4194304 | tf_op jit(solution)/shard_map/all_gather | solution.py:52
  61.3 39.4 %all-gather.5.cloned.1.call-done = bf16[2048,512]{1,0:T(8,128)(2,1)} async-done(((bf16[128,512]{1,0:T(8,128)(2,1)}), bf16[2048,512]{1,0:T(8,128)(2,1)}) %all-gather.5.cloned.1.call-update) | async-done | bytes 2097168 | tf_op jit(solution)/shard_map/all_gather | solution.py:53
  100.7 4.0 %copy.51 = bf16[2048,512]{0,1:T(8,128)(2,1)} copy(bf16[2048,512]{1,0:T(8,128)(2,1)} %all-gather.5.cloned.1.call-done) | data formatting | bytes 4194304 | tf_op jit(solution)/shard_map/all_gather | solution.py:53
  104.7 8.9 %conditional.2 = (f32[1,64,4,4]{1,3,2,0:T(4,128)S(1)}, f32[1,64,2048]{2,1,0:T(8,128)S(1)}) conditional(s32[]{:T(128)} %bitcast.12, () %tuple.29, (s32[2048]{0:T(1024)S(1)}, s32[]{:T(128)}, s32[64]{0:T(128)S(1)}, bf16[2,64,4,4,128]{4,3,2,1,0:T(4,128)(2,1)S(1)}, bf16[2048,4,128]{0,2,1:T(8,128)(2,1)S(1)}, ...), branch_computations={%region_0.0_spmd, %region_1.4_spmd} | conditional | flops 1101134848 | bytes 42238768 | solution.py:71
  105.1 1.7 %fusion = (f32[64,4,4]{0,2,1:T(4,128)S(1)}, f32[4,2048,64,4]{1,2,3,0:T(8,128)S(1)}) fusion(pred[64,2048]{1,0:T(8,128)(4,1)S(1)} %broadcast_compare_fusion, bf16[2,64,4,4,128]{4,1,3,2,0:T(8,128)(2,1)S(1)} %copy.52, bf16[2048,4,128]{0,2,1:T(8,128)(2,1)S(1)} %get-tuple-element.97), kind=kOutput, calls=%fused_computation.2 | convolution fusion | flops 543161344 | bytes 10883072 | tf_op jit(solution)/shard_map/cond/branch_1_fun/tkgd,pkd->tkgp/dot_general | solution.py:12
  106.8 1.9 %fusion.9 = f32[64,4,4,128]{3,0,2,1:T(8,128)S(1)} fusion(bf16[2048,4,128]{0,2,1:T(8,128)(2,1)S(1)} %copy-done, f32[4,2048,64,4]{1,2,3,0:T(8,128)S(1)} %get-tuple-element.106, f32[64,4,4]{0,2,1:T(4,128)S(1)} %broadcast_maximum_fusion, pred[64,2048]{1,0:T(8,128)(4,1)S(1)} %broadcast_compare_fusion), kind=kOutput, calls=%fused_computation.10 | convolution fusion | flops 547356672 | bytes 11145216 | tf_op jit(solution)/shard_map/cond/branch_1_fun/tkgp,pkd->tkgd/dot_general | solution.py:19
  108.7 2.5 %fusion.2 = f32[64,4,4]{0,2,1:T(4,128)S(1)} fusion(f32[4,2048,64,4]{1,2,3,0:T(8,128)S(1)} %get-tuple-element.106, f32[64,4,4]{0,2,1:T(4,128)S(1)} %broadcast_maximum_fusion, pred[64,2048]{1,0:T(8,128)(4,1)S(1)} %broadcast_compare_fusion), kind=kLoop, calls=%fused_computation.4 | loop fusion | flops 10484736 | bytes 8527872 | tf_op jit(solution)/shard_map/cond/branch_1_fun/reduce_sum | solution.py:18
  111.2 1.1 copy.45
  112.4 1.3 stack.31
  113.6 8.0 %conditional.3 = (f32[1,64,4,4]{1,3,2,0:T(4,128)S(1)}, f32[1,64,2048]{2,1,0:T(8,128)}) conditional(s32[]{:T(128)} %bitcast.20, () %tuple.31, (s32[2048]{0:T(1024)S(1)}, s32[]{:T(128)}, s32[64]{0:T(128)S(1)}, bf16[2,64,4,4,128]{4,3,2,1,0:T(4,128)(2,1)S(1)}, bf16[2048,4,128]{0,2,1:T(8,128)(2,1)S(1)}, /*index=5*/bf16[2048,4,128]{0,2,1:T(8,128)(2,1)}) %tuple.56), branch_computations={%region_4.5_spmd, %region_5.8_spmd} | conditional | flops 1101134848 | bytes 42238768 | solution.py:71
  114.1 1.7 %fusion.17 = (f32[64,4,4]{0,2,1:T(4,128)S(1)}, f32[4,2048,64,4]{1,2,3,0:T(8,128)S(1)}) fusion(pred[64,2048]{1,0:T(8,128)(4,1)S(1)} %broadcast_compare_fusion.1, bf16[2,64,4,4,128]{4,1,3,2,0:T(8,128)(2,1)S(1)} %copy.55, bf16[2048,4,128]{0,2,1:T(8,128)(2,1)S(1)} %get-tuple-element.103), kind=kOutput, calls=%fused_computation.20 | convolution fusion | flops 543161344 | bytes 10883072 | tf_op jit(solution)/shard_map/cond/branch_1_fun/tkgd,pkd->tkgp/dot_general | solution.py:12
  115.8 1.9 %fusion.26 = f32[64,4,4,128]{3,0,2,1:T(8,128)S(1)} fusion(bf16[2048,4,128]{0,2,1:T(8,128)(2,1)S(1)} %copy-done.1, f32[4,2048,64,4]{1,2,3,0:T(8,128)S(1)} %get-tuple-element.108, f32[64,4,4]{0,2,1:T(4,128)S(1)} %broadcast_maximum_fusion.1, pred[64,2048]{1,0:T(8,128)(4,1)S(1)} %broadcast_compare_fusion.1), kind=kOutput, calls=%fused_computation.28 | convolution fusion | flops 547356672 | bytes 11145216 | tf_op jit(solution)/shard_map/cond/branch_1_fun/tkgp,pkd->tkgd/dot_general | solution.py:19
  117.8 2.5 %fusion.19 = f32[64,4,4]{0,2,1:T(4,128)S(1)} fusion(f32[4,2048,64,4]{1,2,3,0:T(8,128)S(1)} %get-tuple-element.108, f32[64,4,4]{0,2,1:T(4,128)S(1)} %broadcast_maximum_fusion.1, pred[64,2048]{1,0:T(8,128)(4,1)S(1)} %broadcast_compare_fusion.1), kind=kLoop, calls=%fused_computation.22 | loop fusion | flops 10484736 | bytes 8527872 | tf_op jit(solution)/shard_map/cond/branch_1_fun/reduce_sum | solution.py:18
  120.7 1.0 stack.35
  122.9 1.2 fusion.34
  124.2 11.1 %all_to_all.75 = bf16[2,64,2048]{2,1,0:T(8,128)(2,1)S(1)} all-to-all(bf16[2,64,2048]{2,1,0:T(8,128)(2,1)S(1)} %bitcast.106), channel_id=1, replica_groups=mesh['head'=2,'seq'=16] {'head'}, dimensions={0} | all-to-all | bytes 1048576 | tf_op jit(solution)/shard_map/all_to_all | solution.py:77
  (37 shorter events, 5.0 us)
Async XLA Ops:
  6.5 51.8 %all-gather.3.cloned.1.call-start = ((), (), s32[]{:S(2)}) async-start(), calls=%async_computation.4 | async-start | bytes 2228224 | tf_op jit(solution)/shard_map/all_gather | solution.py:52
  16.1 84.6 %all-gather.5.cloned.1.call-start = ((), (), s32[]{:S(2)}) async-start(), calls=%async_computation.5 | async-start | bytes 2228224 | tf_op jit(solution)/shard_map/all_gather | solution.py:53
  26.5 10.1 %all-to-all-start = ((bf16[64,2,2048]{2,0,1:T(8,128)(2,1)}), bf16[64,2,2048]{2,0,1:T(8,128)(2,1)S(1)}, u32[]{:S(2)}, u32[]{:S(2)}) async-start(bf16[64,2,2048]{2,0,1:T(8,128)(2,1)} %bitcast.98), calls=%async_computation | async-start | bytes 1048576 | tf_op jit(solution)/shard_map/all_to_all | solution.py:31
  105.0 1.7 %copy-start = (bf16[2048,4,128]{0,2,1:T(8,128)(2,1)S(1)}, bf16[2048,4,128]{0,2,1:T(8,128)(2,1)}, u32[]{:S(2)}) copy-start(bf16[2048,4,128]{0,2,1:T(8,128)(2,1)} %get-tuple-element.98) | copy-start | bytes 6291460 | tf_op jit(solution)/shard_map/cond
  114.1 1.7 %copy-start.1 = (bf16[2048,4,128]{0,2,1:T(8,128)(2,1)S(1)}, bf16[2048,4,128]{0,2,1:T(8,128)(2,1)}, u32[]{:S(2)}) copy-start(bf16[2048,4,128]{0,2,1:T(8,128)(2,1)} %get-tuple-element.104) | copy-start | bytes 6291460 | tf_op jit(solution)/shard_map/cond
Sparse Core Ops, SparseCore 0:
  16.2 42.0 all-gather.2
  60.5 40.1 all-gather.4
where the time goes:
time: 144 us; the launch traced here: 143 us
  waiting for transfers between devices  64.6 us (45%)
  blocking collectives  27.2 us (19%)
  local copies, waits for them, and re-layouts  18.5 us (13%)
  between operations  14.8 us (10%)
  matrix products  7.21 us (5%)
  other arithmetic  6.63 us (5%)
  starting transfers between devices  3.53 us (2%)
    all_gather x1, waiting for transfers between devices, on_device(): value_piece = lax.all_gather(v_local, 'seq', axis=0, tiled=True)  39.4 us
    all_gather x1, waiting for transfers between devices, on_device(): key_piece = lax.all_gather(k_local, 'seq', axis=0, tiled=True)  21.2 us
    all_to_all x1, blocking collectives, on_device(): lax.all_to_all(combined, 'head', split_axis=0, concat_axis=1, tiled=True)  11.1 us
    all_to_all x1, blocking collectives, on_device(): lax.all_to_all(keys, 'head', split_axis=1, concat_axis=0, tiled=True)  8.64 us
    all_to_all x1, blocking collectives, on_device(): lax.all_to_all(values, 'head', split_axis=1, concat_axis=0, tiled=True)  7.52 us
    reduce_sum x2, other arithmetic, update_state(): total = jnp.sum(weight, axis=-1)  5.08 us
    all_to_all x1, waiting for transfers between devices, on_device(): lax.all_to_all(queries, 'head', split_axis=1, concat_axis=0, tiled=True)  3.99 us
    all_gather x1, local copies, waits for them, and re-layouts, on_device(): value_piece = lax.all_gather(v_local, 'seq', axis=0, tiled=True)  3.95 us
  transfers between devices with their start and end apart: 3, of which 3 were waited for; matrix products, arithmetic and copies ran while one was open for 5% of the time, Pallas kernels for 0%

commit v1 on v0

--- a/solution.py
+++ b/solution.py
@@ -49,8 +49,11 @@
         jnp.zeros((2, half, kv_local, group, HEAD_DIM), jnp.float32),
     )
     start = jnp.int32(0)
-    key_piece = lax.all_gather(k_local, "seq", axis=0, tiled=True)
-    value_piece = lax.all_gather(v_local, "seq", axis=0, tiled=True)
+    key_piece, value_piece = jnp.split(
+        lax.all_gather(jnp.concatenate([k_local, v_local], 1), "seq", axis=0, tiled=True),
+        [k_local.shape[1]],
+        1,
+    )
     rows = key_piece.shape[0]
     key_piece = key_piece.reshape(rows, kv_local, HEAD_DIM)
     value_piece = value_piece.reshape(rows, kv_local, HEAD_DIM)

time: 144 us -> 124 us (0.86)
  waiting for transfers between devices: 64.6 us -> 46.2 us
  blocking collectives: 27.2 us -> 17.9 us
  starting transfers between devices: 3.53 us -> 7.75 us
  local copies, waits for them, and re-layouts: 18.5 us -> 21.5 us
    all_gather x2 -> x1, waiting for transfers between devices: 60.6 us -> 38.7 us  [on_device(): lax.all_gather(jnp.concatenate([k_local, v_local], 1), 'seq', axis=0, til...]
    split x0 -> x3, local copies, waits for them, and re-layouts: none -> 9.17 us  [on_device(): jnp.split(lax.all_gather(jnp.concatenate([k_local, v_local], 1), 'seq', a...]
    all_to_all x1 -> x0, blocking collectives: 8.64 us -> none  [on_device(): lax.all_to_all(keys, 'head', split_axis=1, concat_axis=0, tiled=True)]
    all_gather x2 -> x0, local copies, waits for them, and re-layouts: 6.88 us -> none  [the longest x1 3.95 us: on_device(): value_piece = lax.all_gather(v_local, 'seq', axis=0, tiled=True)]
    all_to_all x0 -> x1, starting transfers between devices: none -> 4.26 us  [on_device(): lax.all_to_all(keys, 'head', split_axis=1, concat_axis=0, tiled=True)]
    all_to_all x0 -> x1, waiting for transfers between devices: none -> 3.64 us  [on_device(): lax.all_to_all(keys, 'head', split_axis=1, concat_axis=0, tiled=True)]
  transfers between devices with their start and end apart: 3 -> 3, of which waited for: 3 -> 3; matrix products, arithmetic and copies ran while one was open for 5% -> 4% of each run, Pallas kernels for 0% -> 0%
where the time goes in v1:
time: 124 us; the launch traced here: 123 us
  waiting for transfers between devices  46.2 us (37%)
  local copies, waits for them, and re-layouts  21.5 us (17%)
  blocking collectives  17.9 us (14%)
  between operations  14.9 us (12%)
  starting transfers between devices  7.75 us (6%)
  other arithmetic  7.36 us (6%)
  matrix products  7.2 us (6%)
    all_gather x1, waiting for transfers between devices, on_device(): lax.all_gather(jnp.concatenate([k_local, v_local], 1), 'seq', axis=0, til...  38.7 us
    all_to_all x1, blocking collectives, on_device(): lax.all_to_all(combined, 'head', split_axis=0, concat_axis=1, tiled=True)  11.1 us
    split x3, local copies, waits for them, and re-layouts, on_device(): jnp.split(lax.all_gather(jnp.concatenate([k_local, v_local], 1), 'seq', a...  9.17 us
    all_to_all x1, blocking collectives, on_device(): lax.all_to_all(values, 'head', split_axis=1, concat_axis=0, tiled=True)  6.84 us
    reduce_sum x2, other arithmetic, update_state(): total = jnp.sum(weight, axis=-1)  5.08 us
    all_to_all x1, starting transfers between devices, on_device(): lax.all_to_all(keys, 'head', split_axis=1, concat_axis=0, tiled=True)  4.26 us
    dot_general x2, matrix products, update_state(): jnp.einsum('tkgp,pkd->tkgd', weight.astype(jnp.bfloat16), value_piece, pr...  3.86 us
    all_to_all x1, waiting for transfers between devices, on_device(): lax.all_to_all(queries, 'head', split_axis=1, concat_axis=0, tiled=True)  3.8 us
  transfers between devices with their start and end apart: 3, of which 3 were waited for; matrix products, arithmetic and copies ran while one was open for 4% of the time, Pallas kernels for 0%

profile of v1, /device:TPU:0, one launch (start us, length us, event | category | flops | bytes accessed | tf_op | source)
XLA Modules:
  0.0 123.3 jit_solution(15416918690146007499)
XLA Ops:
  6.5 1.6 %copy.81 = bf16[8,2,8,512]{3,2,0,1:T(8,128)(2,1)} copy(bf16[8,2,8,512]{3,2,1,0:T(8,128)(2,1)} %bitcast.112) | data formatting | bytes 262144 | tf_op jit(solution)/shard_map/all_to_all | solution.py:32
  8.1 4.3 %all-to-all-start.1 = ((bf16[64,2,512]{2,0,1:T(8,128)(2,1)}), bf16[64,2,512]{2,0,1:T(8,128)(2,1)S(1)}, u32[]{:S(2)}, u32[]{:S(2)}) async-start(bf16[64,2,512]{2,0,1:T(8,128)(2,1)} %bitcast.100), calls=%async_computation.1 | async-start | bytes 262144 | tf_op jit(solution)/shard_map/all_to_all | solution.py:32
  13.3 3.6 %all-to-all-done.1 = bf16[64,2,512]{2,0,1:T(8,128)(2,1)S(1)} async-done(((bf16[64,2,512]{2,0,1:T(8,128)(2,1)}), bf16[64,2,512]{2,0,1:T(8,128)(2,1)S(1)}, u32[]{:S(2)}, u32[]{:S(2)}) %all-to-all-start.1) | async-done | bytes 131104 | tf_op jit(solution)/shard_map/all_to_all | solution.py:32
  16.9 6.8 %all_to_all.73 = bf16[64,2,512]{2,0,1:T(8,128)(2,1)S(1)} all-to-all(bf16[64,2,512]{2,0,1:T(8,128)(2,1)S(1)} %bitcast.109), channel_id=1, replica_groups=mesh['head'=2,'seq'=16] {'head'}, dimensions={1} | all-to-all | bytes 262144 | tf_op jit(solution)/shard_map/all_to_all | solution.py:33
  24.5 1.9 %copy.79 = bf16[8,2,8,2048]{3,2,0,1:T(8,128)(2,1)} copy(bf16[8,2,8,2048]{3,2,1,0:T(8,128)(2,1)} %bitcast.108) | data formatting | bytes 1048576 | tf_op jit(solution)/shard_map/all_to_all | solution.py:31
  26.4 3.5 %all-to-all-start = ((bf16[64,2,2048]{2,0,1:T(8,128)(2,1)}), bf16[64,2,2048]{2,0,1:T(8,128)(2,1)S(1)}, u32[]{:S(2)}, u32[]{:S(2)}) async-start(bf16[64,2,2048]{2,0,1:T(8,128)(2,1)} %bitcast.98), calls=%async_computation | async-start | bytes 1048576 | tf_op jit(solution)/shard_map/all_to_all | solution.py:31
  32.7 3.8 %all-to-all-done = bf16[64,2,2048]{2,0,1:T(8,128)(2,1)S(1)} async-done(((bf16[64,2,2048]{2,0,1:T(8,128)(2,1)}), bf16[64,2,2048]{2,0,1:T(8,128)(2,1)S(1)}, u32[]{:S(2)}, u32[]{:S(2)}) %all-to-all-start) | async-done | bytes 524320 | tf_op jit(solution)/shard_map/all_to_all | solution.py:31
  37.1 38.7 %all-gather.2.cloned.1.call-done = bf16[2048,1024]{1,0:T(8,128)(2,1)} async-done(((bf16[128,1024]{1,0:T(8,128)(2,1)}), bf16[2048,1024]{1,0:T(8,128)(2,1)}) %all-gather.2.cloned.1.call-update) | async-done | bytes 4194320 | tf_op jit(solution)/shard_map/all_gather | solution.py:53
  75.8 3.8 %fusion.35 = (bf16[2048,512]{1,0:T(8,128)(2,1)S(1)}, bf16[2048,512]{1,0:T(8,128)(2,1)}) fusion(bf16[2048,1024]{1,0:T(8,128)(2,1)} %all-gather.2.cloned.1.call-done), kind=kLoop, calls=%fused_computation.50 | loop fusion | bytes 8388608 | tf_op jit(solution)/shard_map/split | solution.py:52
  79.6 2.4 %copy.51 = bf16[2048,512]{0,1:T(8,128)(2,1)} copy(bf16[2048,512]{1,0:T(8,128)(2,1)S(1)} %get-tuple-element.109) | data formatting | bytes 4194304 | tf_op jit(solution)/shard_map/split | solution.py:52
  82.1 2.9 %copy.50 = bf16[2048,512]{0,1:T(8,128)(2,1)S(1)} copy(bf16[2048,512]{1,0:T(8,128)(2,1)} %get-tuple-element.110) | data formatting | bytes 4194304 | tf_op jit(solution)/shard_map/split | solution.py:52
  85.1 8.9 %conditional.2 = (f32[1,64,4,4]{1,3,2,0:T(4,128)S(1)}, f32[1,64,2048]{2,1,0:T(8,128)S(1)}) conditional(s32[]{:T(128)} %bitcast.12, () %tuple.29, (s32[2048]{0:T(1024)S(1)}, s32[]{:T(128)}, s32[64]{0:T(128)S(1)}, bf16[2,64,4,4,128]{4,3,2,1,0:T(4,128)(2,1)S(1)}, bf16[2048,4,128]{0,2,1:T(8,128)(2,1)S(1)}, ...), branch_computations={%region_0.0_spmd, %region_1.4_spmd} | conditional | flops 1101134848 | bytes 42238768 | solution.py:74
  85.4 1.7 %fusion = (f32[64,4,4]{0,2,1:T(4,128)S(1)}, f32[4,2048,64,4]{1,2,3,0:T(8,128)S(1)}) fusion(pred[64,2048]{1,0:T(8,128)(4,1)S(1)} %broadcast_compare_fusion, bf16[2,64,4,4,128]{4,1,3,2,0:T(8,128)(2,1)S(1)} %copy.52, bf16[2048,4,128]{0,2,1:T(8,128)(2,1)S(1)} %get-tuple-element.97), kind=kOutput, calls=%fused_computation.2 | convolution fusion | flops 543161344 | bytes 10883072 | tf_op jit(solution)/shard_map/cond/branch_1_fun/tkgd,pkd->tkgp/dot_general | solution.py:12
  87.1 1.9 %fusion.9 = f32[64,4,4,128]{3,0,2,1:T(8,128)S(1)} fusion(bf16[2048,4,128]{0,2,1:T(8,128)(2,1)S(1)} %copy-done, f32[4,2048,64,4]{1,2,3,0:T(8,128)S(1)} %get-tuple-element.106, f32[64,4,4]{0,2,1:T(4,128)S(1)} %broadcast_maximum_fusion, pred[64,2048]{1,0:T(8,128)(4,1)S(1)} %broadcast_compare_fusion), kind=kOutput, calls=%fused_computation.10 | convolution fusion | flops 547356672 | bytes 11145216 | tf_op jit(solution)/shard_map/cond/branch_1_fun/tkgp,pkd->tkgd/dot_general | solution.py:19
  89.0 2.5 %fusion.2 = f32[64,4,4]{0,2,1:T(4,128)S(1)} fusion(f32[4,2048,64,4]{1,2,3,0:T(8,128)S(1)} %get-tuple-element.106, f32[64,4,4]{0,2,1:T(4,128)S(1)} %broadcast_maximum_fusion, pred[64,2048]{1,0:T(8,128)(4,1)S(1)} %broadcast_compare_fusion), kind=kLoop, calls=%fused_computation.4 | loop fusion | flops 10484736 | bytes 8527872 | tf_op jit(solution)/shard_map/cond/branch_1_fun/reduce_sum | solution.py:18
  91.6 1.1 copy.45
  92.7 1.3 %stack.31 = f32[1,64,2048]{2,1,0:T(8,128)S(1)} reshape(f32[64,4,4,128]{3,2,1,0:T(4,128)} %copy.45) | data formatting | bytes 1048576 | tf_op jit(solution)/shard_map/stack | solution.py:76
  94.0 8.0 %conditional.3 = (f32[1,64,4,4]{1,3,2,0:T(4,128)S(1)}, f32[1,64,2048]{2,1,0:T(8,128)}) conditional(s32[]{:T(128)} %bitcast.20, () %tuple.31, (s32[2048]{0:T(1024)S(1)}, s32[]{:T(128)}, s32[64]{0:T(128)S(1)}, bf16[2,64,4,4,128]{4,3,2,1,0:T(4,128)(2,1)S(1)}, bf16[2048,4,128]{0,2,1:T(8,128)(2,1)S(1)}, /*index=5*/bf16[2048,4,128]{0,2,1:T(8,128)(2,1)}) %tuple.55), branch_computations={%region_4.5_spmd, %region_5.8_spmd} | conditional | flops 1101134848 | bytes 42238768 | solution.py:74
  94.5 1.7 %fusion.17 = (f32[64,4,4]{0,2,1:T(4,128)S(1)}, f32[4,2048,64,4]{1,2,3,0:T(8,128)S(1)}) fusion(pred[64,2048]{1,0:T(8,128)(4,1)S(1)} %broadcast_compare_fusion.1, bf16[2,64,4,4,128]{4,1,3,2,0:T(8,128)(2,1)S(1)} %copy.55, bf16[2048,4,128]{0,2,1:T(8,128)(2,1)S(1)} %get-tuple-element.103), kind=kOutput, calls=%fused_computation.20 | convolution fusion | flops 543161344 | bytes 10883072 | tf_op jit(solution)/shard_map/cond/branch_1_fun/tkgd,pkd->tkgp/dot_general | solution.py:12
  96.2 1.9 %fusion.26 = f32[64,4,4,128]{3,0,2,1:T(8,128)S(1)} fusion(bf16[2048,4,128]{0,2,1:T(8,128)(2,1)S(1)} %copy-done.1, f32[4,2048,64,4]{1,2,3,0:T(8,128)S(1)} %get-tuple-element.108, f32[64,4,4]{0,2,1:T(4,128)S(1)} %broadcast_maximum_fusion.1, pred[64,2048]{1,0:T(8,128)(4,1)S(1)} %broadcast_compare_fusion.1), kind=kOutput, calls=%fused_computation.28 | convolution fusion | flops 547356672 | bytes 11145216 | tf_op jit(solution)/shard_map/cond/branch_1_fun/tkgp,pkd->tkgd/dot_general | solution.py:19
  98.1 2.5 %fusion.19 = f32[64,4,4]{0,2,1:T(4,128)S(1)} fusion(f32[4,2048,64,4]{1,2,3,0:T(8,128)S(1)} %get-tuple-element.108, f32[64,4,4]{0,2,1:T(4,128)S(1)} %broadcast_maximum_fusion.1, pred[64,2048]{1,0:T(8,128)(4,1)S(1)} %broadcast_compare_fusion.1), kind=kLoop, calls=%fused_computation.22 | loop fusion | flops 10484736 | bytes 8527872 | tf_op jit(solution)/shard_map/cond/branch_1_fun/reduce_sum | solution.py:18
  101.0 1.0 stack.35
  103.2 1.2 fusion.34
  104.5 11.1 %all_to_all.74 = bf16[2,64,2048]{2,1,0:T(8,128)(2,1)S(1)} all-to-all(bf16[2,64,2048]{2,1,0:T(8,128)(2,1)S(1)} %bitcast.106), channel_id=1, replica_groups=mesh['head'=2,'seq'=16] {'head'}, dimensions={0} | all-to-all | bytes 1048576 | tf_op jit(solution)/shard_map/all_to_all | solution.py:80
  (37 shorter events, 6.7 us)
Async XLA Ops:
  8.1 8.8 %all-to-all-start.1 = ((bf16[64,2,512]{2,0,1:T(8,128)(2,1)}), bf16[64,2,512]{2,0,1:T(8,128)(2,1)S(1)}, u32[]{:S(2)}, u32[]{:S(2)}) async-start(bf16[64,2,512]{2,0,1:T(8,128)(2,1)} %bitcast.100), calls=%async_computation.1 | async-start | bytes 262144 | tf_op jit(solution)/shard_map/all_to_all | solution.py:32
  12.4 63.5 %all-gather.2.cloned.1.call-start = ((), (), s32[]{:S(2)}) async-start(), calls=%async_computation.4 | async-start | bytes 4456448 | tf_op jit(solution)/shard_map/all_gather | solution.py:53
  26.4 10.1 %all-to-all-start = ((bf16[64,2,2048]{2,0,1:T(8,128)(2,1)}), bf16[64,2,2048]{2,0,1:T(8,128)(2,1)S(1)}, u32[]{:S(2)}, u32[]{:S(2)}) async-start(bf16[64,2,2048]{2,0,1:T(8,128)(2,1)} %bitcast.98), calls=%async_computation | async-start | bytes 1048576 | tf_op jit(solution)/shard_map/all_to_all | solution.py:31
  85.4 1.7 %copy-start = (bf16[2048,4,128]{0,2,1:T(8,128)(2,1)S(1)}, bf16[2048,4,128]{0,2,1:T(8,128)(2,1)}, u32[]{:S(2)}) copy-start(bf16[2048,4,128]{0,2,1:T(8,128)(2,1)} %get-tuple-element.98) | copy-start | bytes 6291460 | tf_op jit(solution)/shard_map/cond
  94.5 1.7 %copy-start.1 = (bf16[2048,4,128]{0,2,1:T(8,128)(2,1)S(1)}, bf16[2048,4,128]{0,2,1:T(8,128)(2,1)}, u32[]{:S(2)}) copy-start(bf16[2048,4,128]{0,2,1:T(8,128)(2,1)} %get-tuple-element.104) | copy-start | bytes 6291460 | tf_op jit(solution)/shard_map/cond
Sparse Core Ops, SparseCore 0:
  24.6 51.1 all-gather.1
